TPU v7x, 32 devices: a whole 2x2x4 slice. The times are simulated.
32 devices in a mesh: rows: 8 (over z, x), cols: 4 (over y, core).
Axes of the slice: x: 2, y: 2, z: 4, core: 2. Of those that a mesh axis runs over, the one named last changes fastest.
Arguments:
- margins: bfloat16 [8192, 2048], P(('rows', 'cols')), may hold values from -512 to 512
- subset_masks: bfloat16 [8192, 8192], P('rows'), may hold values from 0 to 1
- ridge_param: float32 [], replicated, may hold values from 1024 to 4096
Outputs:
- weights: float32 [8192, 2048], P('rows', 'cols')
- residual_norm: float32 [2048], P('cols')
All inputs are finite; a program needn't handle non-finite values.
Results may differ from a plain program's by a relative error of at most 0.0021.
Values may be sent and summed in bfloat16 or wider, within the bound.
No kernel may reach another device: no remote copies, remote signals or barrier semaphores. Data moves between devices by JAX's collectives and lax.ppermute only.
A program may use at most 128 MiB of HBM per device.

v0:
```python
import jax
import jax.numpy as jnp
from jax import lax
from jax.sharding import PartitionSpec as P

ITERS = 2


def per_device(margins, subset_masks, ridge_param):
    design = subset_masks * 2 - 1
    regrouped = lax.all_to_all(margins, "cols", split_axis=1, concat_axis=0, tiled=True)

    def design_times(operand):
        return lax.dot_general(
            design, operand, (((0,), (0,)), ((), ())), preferred_element_type=jnp.float32
        )

    target = lax.psum_scatter(design_times(regrouped), "rows", scatter_dimension=0, tiled=True)
    first_norms = lax.psum(jnp.sum(target * target, axis=0), "rows")
    weights = jnp.zeros_like(target)
    residual = target
    direction = target
    norm_now = first_norms
    for iteration in range(ITERS):
        dir_low = direction.astype(jnp.bfloat16)
        fitted = jnp.dot(
            design,
            lax.all_gather(dir_low, "rows", axis=0, tiled=True),
            preferred_element_type=jnp.float32,
        )
        fitted_low = fitted.astype(jnp.bfloat16)
        partial_sum = jnp.sum(fitted * fitted_low.astype(jnp.float32), axis=0)
        partial_sum = partial_sum + ridge_param * jnp.sum(
            dir_low.astype(jnp.float32) * direction, axis=0
        )
        curvature = lax.psum(partial_sum, "rows")
        image = (
            lax.psum_scatter(design_times(fitted_low), "rows", scatter_dimension=0, tiled=True)
            + ridge_param * direction
        )
        alpha = norm_now / curvature
        weights = weights + alpha * direction
        residual = residual - alpha * image
        norm_next = lax.psum(jnp.sum(residual * residual, axis=0), "rows")
        if iteration + 1 < ITERS:
            direction = residual + norm_next / norm_now * direction
        norm_now = norm_next
    return (weights, jnp.sqrt(norm_now / first_norms))


def solution(mesh):
    in_specs = (P(("rows", "cols"), None), P("rows", None), P())
    out_specs = (P("rows", "cols"), P("cols"))
    return jax.shard_map(
        per_device, mesh=mesh, in_specs=in_specs, out_specs=out_specs, check_vma=False
    )
```

profile of v0, /device:TPU:0, one launch (start us, length us, event | category | flops | bytes accessed | tf_op | source)
XLA Modules:
  0.0 1246.0 jit_solution(5039856017839600145)
XLA Ops:
  7.2 1.5 copy.5
  8.7 18.5 %all_to_all.19 = bf16[256,4,512]{0,2,1:T(8,128)(2,1)S(1)} all-to-all(bf16[256,4,512]{0,2,1:T(8,128)(2,1)S(1)} %bitcast.9), channel_id=1, replica_groups=mesh['rows'=8,'cols'=4] {'cols'}, dimensions={1} | all-to-all | bytes 2097152 | tf_op jit(solution)/shard_map/all_to_all | solution.py:11
  27.2 0.5 copy.6
  27.7 15.7 %fusion.4 = f32[8192,512]{1,0:T(8,128)} fusion(bf16[1024,512]{1,0:T(8,128)(2,1)S(1)} %bitcast.10, bf16[1024,8192]{1,0:T(8,128)(2,1)} %param.4), kind=kOutput, calls=%fused_computation.15 | convolution fusion | flops 8606711808 | bytes 34603008 | tf_op jit(solution)/shard_map/dot_general | solution.py:14
  43.6 279.9 %reduce-scatter.4.cloned.1.call-done = f32[1024,512]{1,0:T(8,128)} async-done(((f32[8192,512]{1,0:T(8,128)}), f32[1024,512]{1,0:T(8,128)}) %reduce-scatter.4.cloned.1.call-update) | async-done | bytes 2097168 | tf_op jit(solution)/shard_map/reduce_scatter | solution.py:18
  323.5 3.6 multiply_reduce_fusion.4
  327.1 0.2 reduce-scatter.6.cloned.1.call-start
  327.4 123.5 %all-gather.3.cloned.1.call-done = bf16[8192,512]{1,0:T(8,128)(2,1)} async-done(((bf16[1024,512]{1,0:T(8,128)(2,1)}), bf16[8192,512]{1,0:T(8,128)(2,1)}) %all-gather.3.cloned.1.call-update) | async-done | bytes 8388624 | tf_op jit(solution)/shard_map/all_gather | solution.py:28
  450.8 14.8 %multiply_reduce_fusion.5 = (f32[512]{0:T(512)S(1)}, bf16[1024,512]{1,0:T(8,128)(2,1)S(1)}) fusion(bf16[8192,512]{1,0:T(8,128)(2,1)} %all-gather.3.cloned.1.call-done, bf16[1024,8192]{1,0:T(8,128)(2,1)} %param.4), kind=kOutput, calls=%fused_computation.9 | convolution fusion | flops 8609333248 | bytes 26216448 | tf_op jit(solution)/shard_map/dot_general | solution.py:26
  465.6 15.7 %fusion.2 = f32[8192,512]{1,0:T(8,128)} fusion(bf16[1024,8192]{1,0:T(8,128)(2,1)} %param.4, bf16[1024,512]{1,0:T(8,128)(2,1)S(1)} %get-tuple-element.12), kind=kOutput, calls=%fused_computation.13 | convolution fusion | flops 8606711808 | bytes 34603008 | tf_op jit(solution)/shard_map/dot_general | solution.py:14
  482.3 19.3 %all-reduce = (f32[512]{0:T(512)S(1)}, f32[512]{0:T(512)S(1)}) all-reduce(f32[512]{0:T(512)S(1)} %get-tuple-element.3, f32[512]{0:T(512)S(1)} %multiply_add_fusion.9), channel_id=1, replica_groups=mesh['rows'=8,'cols'=4] {'rows'}, use_global_device_ids=true, to_apply=%region_2.0 | all-reduce | flops 1024 | bytes 8192 | tf_op jit(solution)/shard_map/psum | solution.py:19
  501.5 258.0 %reduce-scatter.6.cloned.1.call-done = f32[1024,512]{1,0:T(8,128)} async-done(((f32[8192,512]{1,0:T(8,128)}), f32[1024,512]{1,0:T(8,128)}) %reduce-scatter.6.cloned.1.call-update) | async-done | bytes 2097168 | tf_op jit(solution)/shard_map/reduce_scatter | solution.py:38
  759.5 2.0 multiply_reduce_fusion.3
  761.6 19.5 %psum.37 = f32[512]{0:T(512)S(1)} all-reduce(f32[512]{0:T(512)S(1)} %multiply_reduce_fusion.3), channel_id=1, replica_groups=mesh['rows'=8,'cols'=4] {'rows'}, use_global_device_ids=true, to_apply=%region_8.0 | all-reduce | flops 512 | bytes 4096 | tf_op jit(solution)/shard_map/psum | solution.py:44
  781.0 3.2 multiply_reduce_fusion.1
  784.2 0.3 reduce-scatter.8.cloned.1.call-start
  784.5 121.6 %all-gather.5.cloned.1.call-done = bf16[8192,512]{1,0:T(8,128)(2,1)} async-done(((bf16[1024,512]{1,0:T(8,128)(2,1)}), bf16[8192,512]{1,0:T(8,128)(2,1)}) %all-gather.5.cloned.1.call-update) | async-done | bytes 8388624 | tf_op jit(solution)/shard_map/all_gather | solution.py:28
  906.1 14.8 %multiply_reduce_fusion.2 = (f32[512]{0:T(512)S(1)}, bf16[1024,512]{1,0:T(8,128)(2,1)S(1)}) fusion(bf16[8192,512]{1,0:T(8,128)(2,1)} %all-gather.5.cloned.1.call-done, bf16[1024,8192]{1,0:T(8,128)(2,1)} %param.4), kind=kOutput, calls=%fused_computation.4 | convolution fusion | flops 8609333248 | bytes 26216448 | tf_op jit(solution)/shard_map/dot_general | solution.py:26
  920.9 15.7 %fusion = f32[8192,512]{1,0:T(8,128)} fusion(bf16[1024,8192]{1,0:T(8,128)(2,1)} %param.4, bf16[1024,512]{1,0:T(8,128)(2,1)S(1)} %get-tuple-element.14), kind=kOutput, calls=%fused_computation.11 | convolution fusion | flops 8606711808 | bytes 34603008 | tf_op jit(solution)/shard_map/dot_general | solution.py:14
  936.7 19.3 %psum.38 = f32[512]{0:T(512)S(1)} all-reduce(f32[512]{0:T(512)S(1)} %multiply_add_fusion.8), channel_id=1, replica_groups=mesh['rows'=8,'cols'=4] {'rows'}, use_global_device_ids=true, to_apply=%region_11.0 | all-reduce | flops 512 | bytes 4096 | tf_op jit(solution)/shard_map/psum | solution.py:36
  956.0 258.9 %reduce-scatter.8.cloned.1.call-done = f32[1024,512]{1,0:T(8,128)} async-done(((f32[8192,512]{1,0:T(8,128)}), f32[1024,512]{1,0:T(8,128)}) %reduce-scatter.8.cloned.1.call-update) | async-done | bytes 2097168 | tf_op jit(solution)/shard_map/reduce_scatter | solution.py:38
  1214.9 4.6 multiply_reduce_fusion
  1219.4 19.5 %psum.39 = f32[512]{0:T(512)S(1)} all-reduce(f32[512]{0:T(512)S(1)} %get-tuple-element.7), channel_id=1, replica_groups=mesh['rows'=8,'cols'=4] {'rows'}, use_global_device_ids=true, to_apply=%region_14.0 | all-reduce | flops 512 | bytes 4096 | tf_op jit(solution)/shard_map/psum | solution.py:44
  1238.9 0.6 divide_sqrt_fusion
  (15 shorter events, 0.2 us)
Async XLA Ops:
  7.2 316.3 %reduce-scatter.4.cloned.1.call-start = ((), (), s32[]{:S(2)}) async-start(), calls=%async_computation.4 | async-start | bytes 18874368 | tf_op jit(solution)/shard_map/reduce_scatter | solution.py:18
  43.5 407.3 %all-gather.3.cloned.1.call-start = ((), (), s32[]{:S(2)}) async-start(), calls=%async_computation.5 | async-start | bytes 9437184 | tf_op jit(solution)/shard_map/all_gather | solution.py:28
  327.1 432.4 %reduce-scatter.6.cloned.1.call-start = ((), (), s32[]{:S(2)}) async-start(), calls=%async_computation.6 | async-start | bytes 18874368 | tf_op jit(solution)/shard_map/reduce_scatter | solution.py:38
  481.4 278.1 %copy-start = (f32[1024,512]{1,0:T(8,128)S(1)}, f32[1024,512]{1,0:T(8,128)}, u32[]{:S(2)}) copy-start(f32[1024,512]{1,0:T(8,128)} %reduce-scatter.4.cloned.1.call-done) | copy-start | bytes 6291460
  481.4 424.7 %all-gather.5.cloned.1.call-start = ((), (), s32[]{:S(2)}) async-start(), calls=%async_computation.7 | async-start | bytes 9437184 | tf_op jit(solution)/shard_map/all_gather | solution.py:28
  784.2 430.7 %reduce-scatter.8.cloned.1.call-start = ((), (), s32[]{:S(2)}) async-start(), calls=%async_computation.8 | async-start | bytes 18874368 | tf_op jit(solution)/shard_map/reduce_scatter | solution.py:38
Sparse Core Ops, SparseCore 0:
  43.6 279.8 reduce-scatter.3
  327.2 123.5 all-gather.2
  481.5 277.9 reduce-scatter.5
  784.3 121.7 all-gather.4
  936.8 278.0 reduce-scatter.7
where the time goes:
time: 1250 us
  waiting for transfers between devices  1040 us (83%)
  blocking collectives  96 us (8%)
  matrix products  76.8 us (6%)
  between operations  14.6 us (1%)
  other arithmetic  14 us (1%)
    reduce_scatter x2, waiting for transfers between devices, per_device(): lax.psum_scatter(design_times(fitted_low), 'rows', scatter_dimension=0, t...  517 us
    reduce_scatter x1, waiting for transfers between devices, per_device(): lax.psum_scatter(design_times(regrouped), 'rows', scatter_dimension=0, ti...  280 us
    all_gather x2, waiting for transfers between devices, per_device(): lax.all_gather(dir_low, 'rows', axis=0, tiled=True)  245 us
    dot_general x3, matrix products, design_times(): lax.dot_general(design, operand, (((0,), (0,)), ((), ())), preferred_elem...  47.2 us
    psum x2, blocking collectives, per_device(): norm_next = lax.psum(jnp.sum(residual * residual, axis=0), 'rows')  38.9 us
    dot_general x2, matrix products, per_device(): jnp.dot(design, lax.all_gather(dir_low, 'rows', axis=0, tiled=True), pref...  29.6 us
  transfers between devices with their start and end apart: 5, of which 5 were waited for; matrix products, arithmetic and copies ran while one was open for 0% of the time, Pallas kernels for 0%

commit v1 on v0

--- a/solution.py
+++ b/solution.py
@@ -4,6 +4,27 @@
 from jax.sharding import PartitionSpec as P
 
 ITERS = 2
+
+
+def gather_around(array, axis, dim):
+    length, position, rows = (lax.axis_size(axis), lax.axis_index(axis), array.shape[dim])
+    right = [(i, (i + 1) % length) for i in range(length)]
+    backward = [(i, (i - 1) % length) for i in range(length)]
+    whole = jnp.zeros((*array.shape[:dim], length * rows, *array.shape[dim + 1 :]), array.dtype)
+    whole = lax.dynamic_update_slice_in_dim(whole, array, position * rows, axis=dim)
+    from_left = from_right = array
+    halfway = length // 2
+    for step in range(1, halfway + 1):
+        from_left = lax.ppermute(from_left, axis, right)
+        whole = lax.dynamic_update_slice_in_dim(
+            whole, from_left, (position - step) % length * rows, axis=dim
+        )
+        if step < length - halfway:
+            from_right = lax.ppermute(from_right, axis, backward)
+            whole = lax.dynamic_update_slice_in_dim(
+                whole, from_right, (position + step) % length * rows, axis=dim
+            )
+    return whole
 
 
 def per_device(margins, subset_masks, ridge_param):
@@ -24,9 +45,7 @@
     for iteration in range(ITERS):
         dir_low = direction.astype(jnp.bfloat16)
         fitted = jnp.dot(
-            design,
-            lax.all_gather(dir_low, "rows", axis=0, tiled=True),
-            preferred_element_type=jnp.float32,
+            design, gather_around(dir_low, "rows", 0), preferred_element_type=jnp.float32
         )
         fitted_low = fitted.astype(jnp.bfloat16)
         partial_sum = jnp.sum(fitted * fitted_low.astype(jnp.float32), axis=0)

time: 1250 us -> 1320 us (1.056)
  starting transfers between devices: 0.61 us -> 68.2 us
    ppermute x0 -> x14, waiting for transfers between devices: none -> 251 us  [the longest x8 212 us: gather_around(): from_left = lax.ppermute(from_left, axis, right)]
    all_gather x2 -> x0, waiting for transfers between devices: 245 us -> none  [per_device(): lax.all_gather(dir_low, 'rows', axis=0, tiled=True)]
    ppermute x0 -> x14, starting transfers between devices: none -> 68.1 us  [the longest x6 56.5 us: gather_around(): from_right = lax.ppermute(from_right, axis, backward)]
  transfers between devices with their start and end apart: 5 -> 17, of which waited for: 5 -> 13; matrix products, arithmetic and copies ran while one was open for 0% -> 0% of each run, Pallas kernels for 0% -> 0%
where the time goes in v1:
time: 1320 us
  waiting for transfers between devices  1050 us (80%)
  blocking collectives  95.2 us (7%)
  matrix products  72.2 us (5%)
  starting transfers between devices  68.2 us (5%)
  between operations  14.7 us (1%)
    reduce_scatter x2, waiting for transfers between devices, per_device(): lax.psum_scatter(design_times(fitted_low), 'rows', scatter_dimension=0, t...  518 us
    reduce_scatter x1, waiting for transfers between devices, per_device(): lax.psum_scatter(design_times(regrouped), 'rows', scatter_dimension=0, ti...  280 us
    ppermute x8, waiting for transfers between devices, gather_around(): from_left = lax.ppermute(from_left, axis, right)  212 us
    ppermute x6, starting transfers between devices, gather_around(): from_right = lax.ppermute(from_right, axis, backward)  56.5 us
    dot_general x3, matrix products, design_times(): lax.dot_general(design, operand, (((0,), (0,)), ((), ())), preferred_elem...  47.3 us
    ppermute x6, waiting for transfers between devices, gather_around(): from_right = lax.ppermute(from_right, axis, backward)  39.3 us
    psum x2, blocking collectives, per_device(): norm_next = lax.psum(jnp.sum(residual * residual, axis=0), 'rows')  39 us
  transfers between devices with their start and end apart: 17, of which 13 were waited for; matrix products, arithmetic and copies ran while one was open for 0% of the time, Pallas kernels for 0%

profile of v1, /device:TPU:0, one launch (start us, length us, event | category | flops | bytes accessed | tf_op | source)
XLA Modules:
  0.0 1321.7 jit_solution(15967224766533010931)
XLA Ops:
  8.7 18.5 %all_to_all.19 = bf16[256,4,512]{0,2,1:T(8,128)(2,1)S(1)} all-to-all(bf16[256,4,512]{0,2,1:T(8,128)(2,1)S(1)} %bitcast.9), channel_id=1, replica_groups=mesh['rows'=8,'cols'=4] {'cols'}, dimensions={1} | all-to-all | bytes 2097152 | tf_op jit(solution)/shard_map/all_to_all | solution.py:32
  27.7 15.7 %fusion.4 = f32[8192,512]{1,0:T(8,128)} fusion(bf16[1024,512]{1,0:T(8,128)(2,1)S(1)} %bitcast.10, bf16[1024,8192]{1,0:T(8,128)(2,1)} %param.4), kind=kOutput, calls=%fused_computation.15 | convolution fusion | flops 8606711808 | bytes 34603008 | tf_op jit(solution)/shard_map/dot_general | solution.py:35
  43.6 279.9 %reduce-scatter.4.cloned.1.call-done = f32[1024,512]{1,0:T(8,128)} async-done(((f32[8192,512]{1,0:T(8,128)}), f32[1024,512]{1,0:T(8,128)}) %reduce-scatter.4.cloned.1.call-update) | async-done | bytes 2097168 | tf_op jit(solution)/shard_map/reduce_scatter | solution.py:39
  331.0 40.5 %collective-permute-done = bf16[1024,512]{1,0:T(8,128)(2,1)S(1)} collective-permute-done((bf16[1024,512]{1,0:T(8,128)(2,1)S(1)}, bf16[1024,512]{1,0:T(8,128)(2,1)S(1)}, u32[]{:S(2)}, u32[]{:S(2)}) %collective-permute-start) | collective-permute-done | bytes 1048608 | tf_op jit(solution)/shard_map/ppermute | solution.py:18
  376.2 22.6 %collective-permute-done.2 = bf16[1024,512]{1,0:T(8,128)(2,1)S(1)} collective-permute-done((bf16[1024,512]{1,0:T(8,128)(2,1)S(1)}, bf16[1024,512]{1,0:T(8,128)(2,1)S(1)}, u32[]{:S(2)}, u32[]{:S(2)}) %collective-permute-start.2) | collective-permute-done | bytes 1048608 | tf_op jit(solution)/shard_map/ppermute | solution.py:18
  398.8 21.0 %collective-permute-done.3 = bf16[1024,512]{1,0:T(8,128)(2,1)} collective-permute-done((bf16[1024,512]{1,0:T(8,128)(2,1)S(1)}, bf16[1024,512]{1,0:T(8,128)(2,1)}, u32[]{:S(2)}, u32[]{:S(2)}) %collective-permute-start.3) | collective-permute-done | bytes 1048608 | tf_op jit(solution)/shard_map/ppermute | solution.py:23
  423.9 20.9 %collective-permute-done.4 = bf16[1024,512]{1,0:T(8,128)(2,1)} collective-permute-done((bf16[1024,512]{1,0:T(8,128)(2,1)S(1)}, bf16[1024,512]{1,0:T(8,128)(2,1)}, u32[]{:S(2)}, u32[]{:S(2)}) %collective-permute-start.4) | collective-permute-done | bytes 1048608 | tf_op jit(solution)/shard_map/ppermute | solution.py:18
  448.9 18.2 %collective-permute-done.5 = bf16[1024,512]{1,0:T(8,128)(2,1)} collective-permute-done((bf16[1024,512]{1,0:T(8,128)(2,1)}, bf16[1024,512]{1,0:T(8,128)(2,1)}, u32[]{:S(2)}, u32[]{:S(2)}) %collective-permute-start.5) | collective-permute-done | bytes 1048608 | tf_op jit(solution)/shard_map/ppermute | solution.py:23
  468.5 21.5 %collective-permute-done.6 = bf16[1024,512]{1,0:T(8,128)(2,1)} collective-permute-done((bf16[1024,512]{1,0:T(8,128)(2,1)}, bf16[1024,512]{1,0:T(8,128)(2,1)}, u32[]{:S(2)}, u32[]{:S(2)}) %collective-permute-start.6) | collective-permute-done | bytes 1048608 | tf_op jit(solution)/shard_map/ppermute | solution.py:18
  503.7 15.8 %fusion.2 = f32[8192,512]{1,0:T(8,128)} fusion(bf16[1024,8192]{1,0:T(8,128)(2,1)} %param.4, bf16[1024,512]{1,0:T(8,128)(2,1)S(1)} %get-tuple-element.12), kind=kOutput, calls=%fused_computation.13 | convolution fusion | flops 8606711808 | bytes 34603008 | tf_op jit(solution)/shard_map/dot_general | solution.py:35
  520.4 19.9 %all-reduce = (f32[512]{0:T(512)S(1)}, f32[512]{0:T(512)S(1)}) all-reduce(f32[512]{0:T(512)S(1)} %get-tuple-element.3, f32[512]{0:T(512)S(1)} %multiply_add_fusion.9), channel_id=1, replica_groups=mesh['rows'=8,'cols'=4] {'rows'}, use_global_device_ids=true, to_apply=%region_2.0 | all-reduce | flops 1024 | bytes 8192 | tf_op jit(solution)/shard_map/psum | solution.py:40
  540.2 258.5 %reduce-scatter.6.cloned.1.call-done = f32[1024,512]{1,0:T(8,128)} async-done(((f32[8192,512]{1,0:T(8,128)}), f32[1024,512]{1,0:T(8,128)}) %reduce-scatter.6.cloned.1.call-update) | async-done | bytes 2097168 | tf_op jit(solution)/shard_map/reduce_scatter | solution.py:57
  800.8 19.5 %psum.37 = f32[512]{0:T(512)S(1)} all-reduce(f32[512]{0:T(512)S(1)} %multiply_reduce_fusion.3), channel_id=1, replica_groups=mesh['rows'=8,'cols'=4] {'rows'}, use_global_device_ids=true, to_apply=%region_8.9 | all-reduce | flops 512 | bytes 4096 | tf_op jit(solution)/shard_map/psum | solution.py:63
  827.3 36.9 %collective-permute-done.7 = bf16[1024,512]{1,0:T(8,128)(2,1)S(1)} collective-permute-done((bf16[1024,512]{1,0:T(8,128)(2,1)S(1)}, bf16[1024,512]{1,0:T(8,128)(2,1)S(1)}, u32[]{:S(2)}, u32[]{:S(2)}) %collective-permute-start.7) | collective-permute-done | bytes 1048608 | tf_op jit(solution)/shard_map/ppermute | solution.py:18
  866.7 20.8 %collective-permute-start.10 = (bf16[1024,512]{1,0:T(8,128)(2,1)S(1)}, bf16[1024,512]{1,0:T(8,128)(2,1)S(1)}, u32[]{:S(2)}, u32[]{:S(2)}) collective-permute-start(bf16[1024,512]{1,0:T(8,128)(2,1)S(1)} %collective-permute-done.8), channel_id=1, source_target_pairs={{0,28},{4,0},{8,4},{12,8},{16,12},{20,16},{24,20},{28,24},{1,29},{... | collective-permute-start | bytes 3145736 | tf_op jit(solution)/shard_map/ppermute | solution.py:23
  887.5 23.7 %collective-permute-done.9 = bf16[1024,512]{1,0:T(8,128)(2,1)S(1)} collective-permute-done((bf16[1024,512]{1,0:T(8,128)(2,1)S(1)}, bf16[1024,512]{1,0:T(8,128)(2,1)S(1)}, u32[]{:S(2)}, u32[]{:S(2)}) %collective-permute-start.9) | collective-permute-done | bytes 1048608 | tf_op jit(solution)/shard_map/ppermute | solution.py:18
  913.7 21.4 %collective-permute-start.12 = (bf16[1024,512]{1,0:T(8,128)(2,1)S(1)}, bf16[1024,512]{1,0:T(8,128)(2,1)S(1)}, u32[]{:S(2)}, u32[]{:S(2)}) collective-permute-start(bf16[1024,512]{1,0:T(8,128)(2,1)S(1)} %collective-permute-done.10), channel_id=1, source_target_pairs={{0,28},{4,0},{8,4},{12,8},{16,12},{20,16},{24,20},{28,24},{1,29},{... | collective-permute-start | bytes 3145736 | tf_op jit(solution)/shard_map/ppermute | solution.py:23
  935.1 22.8 %collective-permute-done.11 = bf16[1024,512]{1,0:T(8,128)(2,1)S(1)} collective-permute-done((bf16[1024,512]{1,0:T(8,128)(2,1)S(1)}, bf16[1024,512]{1,0:T(8,128)(2,1)S(1)}, u32[]{:S(2)}, u32[]{:S(2)}) %collective-permute-start.11) | collective-permute-done | bytes 1048608 | tf_op jit(solution)/shard_map/ppermute | solution.py:18
  961.7 23.0 %collective-permute-done.13 = bf16[1024,512]{1,0:T(8,128)(2,1)S(1)} collective-permute-done((bf16[1024,512]{1,0:T(8,128)(2,1)S(1)}, bf16[1024,512]{1,0:T(8,128)(2,1)S(1)}, u32[]{:S(2)}, u32[]{:S(2)}) %collective-permute-start.13) | collective-permute-done | bytes 1048608 | tf_op jit(solution)/shard_map/ppermute | solution.py:18
  984.8 12.6 multiply_reduce_fusion.2
  997.4 15.8 %fusion = f32[8192,512]{1,0:T(8,128)} fusion(bf16[1024,8192]{1,0:T(8,128)(2,1)} %param.4, bf16[1024,512]{1,0:T(8,128)(2,1)S(1)} %get-tuple-element.14), kind=kOutput, calls=%fused_computation.11 | convolution fusion | flops 8606711808 | bytes 34603008 | tf_op jit(solution)/shard_map/dot_general | solution.py:35
  1013.2 17.9 %psum.38 = f32[512]{0:T(512)S(1)} all-reduce(f32[512]{0:T(512)S(1)} %multiply_add_fusion.8), channel_id=1, replica_groups=mesh['rows'=8,'cols'=4] {'rows'}, use_global_device_ids=true, to_apply=%region_11.12 | all-reduce | flops 512 | bytes 4096 | tf_op jit(solution)/shard_map/psum | solution.py:55
  1031.1 259.4 %reduce-scatter.8.cloned.1.call-done = f32[1024,512]{1,0:T(8,128)} async-done(((f32[8192,512]{1,0:T(8,128)}), f32[1024,512]{1,0:T(8,128)}) %reduce-scatter.8.cloned.1.call-update) | async-done | bytes 2097168 | tf_op jit(solution)/shard_map/reduce_scatter | solution.py:57
  1295.1 19.5 %psum.39 = f32[512]{0:T(512)S(1)} all-reduce(f32[512]{0:T(512)S(1)} %get-tuple-element.9), channel_id=1, replica_groups=mesh['rows'=8,'cols'=4] {'rows'}, use_global_device_ids=true, to_apply=%region_14.15 | all-reduce | flops 512 | bytes 4096 | tf_op jit(solution)/shard_map/psum | solution.py:63
  (59 shorter events, 60.7 us)
Async XLA Ops:
  7.2 316.3 %reduce-scatter.4.cloned.1.call-start = ((), (), s32[]{:S(2)}) async-start(), calls=%async_computation.4 | async-start | bytes 18874368 | tf_op jit(solution)/shard_map/reduce_scatter | solution.py:39
  43.5 755.2 %reduce-scatter.6.cloned.1.call-start = ((), (), s32[]{:S(2)}) async-start(), calls=%async_computation.5 | async-start | bytes 18874368 | tf_op jit(solution)/shard_map/reduce_scatter | solution.py:57
  326.2 45.3 %collective-permute-start = (bf16[1024,512]{1,0:T(8,128)(2,1)S(1)}, bf16[1024,512]{1,0:T(8,128)(2,1)S(1)}, u32[]{:S(2)}, u32[]{:S(2)}) collective-permute-start(bf16[1024,512]{1,0:T(8,128)(2,1)S(1)} %get-tuple-element.8), channel_id=1, source_target_pairs={{0,4},{4,8},{8,12},{12,16},{16,20},{20,24},{24,28},{28,0},{1,5},{5... | collective-permute-start | bytes 3145736 | tf_op jit(solution)/shard_map/ppermute | solution.py:18
  327.7 46.2 %collective-permute-start.1 = (bf16[1024,512]{1,0:T(8,128)(2,1)S(1)}, bf16[1024,512]{1,0:T(8,128)(2,1)S(1)}, u32[]{:S(2)}, u32[]{:S(2)}) collective-permute-start(bf16[1024,512]{1,0:T(8,128)(2,1)S(1)} %get-tuple-element.8), channel_id=1, source_target_pairs={{0,28},{4,0},{8,4},{12,8},{16,12},{20,16},{24,20},{28,24},{1,29},{... | collective-permute-start | bytes 3145736 | tf_op jit(solution)/shard_map/ppermute | solution.py:23
  371.5 27.3 %collective-permute-start.2 = (bf16[1024,512]{1,0:T(8,128)(2,1)S(1)}, bf16[1024,512]{1,0:T(8,128)(2,1)S(1)}, u32[]{:S(2)}, u32[]{:S(2)}) collective-permute-start(bf16[1024,512]{1,0:T(8,128)(2,1)S(1)} %collective-permute-done), channel_id=1, source_target_pairs={{0,4},{4,8},{8,12},{12,16},{16,20},{20,24},{24,28},{28,0},{1,5},{5... | collective-permute-start | bytes 3145736 | tf_op jit(solution)/shard_map/ppermute | solution.py:18
  373.9 45.9 %collective-permute-start.3 = (bf16[1024,512]{1,0:T(8,128)(2,1)S(1)}, bf16[1024,512]{1,0:T(8,128)(2,1)}, u32[]{:S(2)}, u32[]{:S(2)}) collective-permute-start(bf16[1024,512]{1,0:T(8,128)(2,1)S(1)} %collective-permute-done.1), channel_id=1, source_target_pairs={{0,28},{4,0},{8,4},{12,8},{16,12},{20,16},{24,20},{28,24},{1,29},{... | collective-permute-start | bytes 3145736 | tf_op jit(solution)/shard_map/ppermute | solution.py:23
  398.8 21.0 %copy-start.1 = (bf16[1024,512]{1,0:T(8,128)(2,1)}, bf16[1024,512]{1,0:T(8,128)(2,1)S(1)}, u32[]{:S(2)}) copy-start(bf16[1024,512]{1,0:T(8,128)(2,1)S(1)} %collective-permute-done.2) | copy-start | bytes 3145732
  398.8 46.0 %collective-permute-start.4 = (bf16[1024,512]{1,0:T(8,128)(2,1)S(1)}, bf16[1024,512]{1,0:T(8,128)(2,1)}, u32[]{:S(2)}, u32[]{:S(2)}) collective-permute-start(bf16[1024,512]{1,0:T(8,128)(2,1)S(1)} %collective-permute-done.2), channel_id=1, source_target_pairs={{0,4},{4,8},{8,12},{12,16},{16,20},{20,24},{24,28},{28,0},{1,5},{5... | collective-permute-start | bytes 3145736 | tf_op jit(solution)/shard_map/ppermute | solution.py:18
  419.8 47.3 %collective-permute-start.5 = (bf16[1024,512]{1,0:T(8,128)(2,1)}, bf16[1024,512]{1,0:T(8,128)(2,1)}, u32[]{:S(2)}, u32[]{:S(2)}) collective-permute-start(bf16[1024,512]{1,0:T(8,128)(2,1)} %collective-permute-done.3), channel_id=1, source_target_pairs={{0,28},{4,0},{8,4},{12,8},{16,12},{20,16},{24,20},{28,24},{1,29},{... | collective-permute-start | bytes 3145736 | tf_op jit(solution)/shard_map/ppermute | solution.py:23
  444.8 45.2 %collective-permute-start.6 = (bf16[1024,512]{1,0:T(8,128)(2,1)}, bf16[1024,512]{1,0:T(8,128)(2,1)}, u32[]{:S(2)}, u32[]{:S(2)}) collective-permute-start(bf16[1024,512]{1,0:T(8,128)(2,1)} %collective-permute-done.4), channel_id=1, source_target_pairs={{0,4},{4,8},{8,12},{12,16},{16,20},{20,24},{24,28},{28,0},{1,5},{5... | collective-permute-start | bytes 3145736 | tf_op jit(solution)/shard_map/ppermute | solution.py:18
  444.9 1.2 copy-start.2
  519.5 279.3 %copy-start = (f32[1024,512]{1,0:T(8,128)S(1)}, f32[1024,512]{1,0:T(8,128)}, u32[]{:S(2)}) copy-start(f32[1024,512]{1,0:T(8,128)} %reduce-scatter.4.cloned.1.call-done) | copy-start | bytes 6291460
  519.5 771.0 %reduce-scatter.8.cloned.1.call-start = ((), (), s32[]{:S(2)}) async-start(), calls=%async_computation.6 | async-start | bytes 18874368 | tf_op jit(solution)/shard_map/reduce_scatter | solution.py:57
  822.5 41.7 %collective-permute-start.7 = (bf16[1024,512]{1,0:T(8,128)(2,1)S(1)}, bf16[1024,512]{1,0:T(8,128)(2,1)S(1)}, u32[]{:S(2)}, u32[]{:S(2)}) collective-permute-start(bf16[1024,512]{1,0:T(8,128)(2,1)S(1)} %get-tuple-element.7), channel_id=1, source_target_pairs={{0,4},{4,8},{8,12},{12,16},{16,20},{20,24},{24,28},{28,0},{1,5},{5... | collective-permute-start | bytes 3145736 | tf_op jit(solution)/shard_map/ppermute | solution.py:18
  822.6 44.1 %collective-permute-start.8 = (bf16[1024,512]{1,0:T(8,128)(2,1)S(1)}, bf16[1024,512]{1,0:T(8,128)(2,1)S(1)}, u32[]{:S(2)}, u32[]{:S(2)}) collective-permute-start(bf16[1024,512]{1,0:T(8,128)(2,1)S(1)} %get-tuple-element.7), channel_id=1, source_target_pairs={{0,28},{4,0},{8,4},{12,8},{16,12},{20,16},{24,20},{28,24},{1,29},{... | collective-permute-start | bytes 3145736 | tf_op jit(solution)/shard_map/ppermute | solution.py:23
  864.2 47.0 %collective-permute-start.9 = (bf16[1024,512]{1,0:T(8,128)(2,1)S(1)}, bf16[1024,512]{1,0:T(8,128)(2,1)S(1)}, u32[]{:S(2)}, u32[]{:S(2)}) collective-permute-start(bf16[1024,512]{1,0:T(8,128)(2,1)S(1)} %collective-permute-done.7), channel_id=1, source_target_pairs={{0,4},{4,8},{8,12},{12,16},{16,20},{20,24},{24,28},{28,0},{1,5},{5... | collective-permute-start | bytes 3145736 | tf_op jit(solution)/shard_map/ppermute | solution.py:18
  866.7 47.0 %collective-permute-start.10 = (bf16[1024,512]{1,0:T(8,128)(2,1)S(1)}, bf16[1024,512]{1,0:T(8,128)(2,1)S(1)}, u32[]{:S(2)}, u32[]{:S(2)}) collective-permute-start(bf16[1024,512]{1,0:T(8,128)(2,1)S(1)} %collective-permute-done.8), channel_id=1, source_target_pairs={{0,28},{4,0},{8,4},{12,8},{16,12},{20,16},{24,20},{28,24},{1,29},{... | collective-permute-start | bytes 3145736 | tf_op jit(solution)/shard_map/ppermute | solution.py:23
  911.2 46.6 %collective-permute-start.11 = (bf16[1024,512]{1,0:T(8,128)(2,1)S(1)}, bf16[1024,512]{1,0:T(8,128)(2,1)S(1)}, u32[]{:S(2)}, u32[]{:S(2)}) collective-permute-start(bf16[1024,512]{1,0:T(8,128)(2,1)S(1)} %collective-permute-done.9), channel_id=1, source_target_pairs={{0,4},{4,8},{8,12},{12,16},{16,20},{20,24},{24,28},{28,0},{1,5},{5... | collective-permute-start | bytes 3145736 | tf_op jit(solution)/shard_map/ppermute | solution.py:18
  913.7 47.9 %collective-permute-start.12 = (bf16[1024,512]{1,0:T(8,128)(2,1)S(1)}, bf16[1024,512]{1,0:T(8,128)(2,1)S(1)}, u32[]{:S(2)}, u32[]{:S(2)}) collective-permute-start(bf16[1024,512]{1,0:T(8,128)(2,1)S(1)} %collective-permute-done.10), channel_id=1, source_target_pairs={{0,28},{4,0},{8,4},{12,8},{16,12},{20,16},{24,20},{28,24},{1,29},{... | collective-permute-start | bytes 3145736 | tf_op jit(solution)/shard_map/ppermute | solution.py:23
  957.8 26.9 %collective-permute-start.13 = (bf16[1024,512]{1,0:T(8,128)(2,1)S(1)}, bf16[1024,512]{1,0:T(8,128)(2,1)S(1)}, u32[]{:S(2)}, u32[]{:S(2)}) collective-permute-start(bf16[1024,512]{1,0:T(8,128)(2,1)S(1)} %collective-permute-done.11), channel_id=1, source_target_pairs={{0,4},{4,8},{8,12},{12,16},{16,20},{20,24},{24,28},{28,0},{1,5},{5... | collective-permute-start | bytes 3145736 | tf_op jit(solution)/shard_map/ppermute | solution.py:18
Sparse Core Ops, SparseCore 0:
  43.6 279.8 reduce-scatter.3
  519.6 279.0 reduce-scatter.5
  1013.3 277.1 reduce-scatter.7
